TPU v7x, 256 devices: a 4x2x16 block of a 4x16x16 slice. The times are simulated.
256 devices in a mesh: groups: 2 (over y), row: 16 (over z), col: 4 (over x), sub: 2 (over core).
Axes of the slice: x: 4, y: 2, z: 16, core: 2. Of those that a mesh axis runs over, the one named last changes fastest.
The devices are a block of a 4x16x16 slice.
Arguments:
- saved_alignment: bfloat16 [64, 1024, 256], P(('col', 'sub'), ('groups', 'row')), parts along dimension 1, may hold values from -6 to 6
- homolog_existence: int32 [64, 1024], P(('col', 'sub'), ('groups', 'row')), parts along dimension 1, may hold values 0 or 1
- amino_existence: int32 [1024], P(('groups', 'row')), parts along dimension 0, may hold values 0 or 1
- couple_delta_adjoint: bfloat16 [1024, 512, 128], P(('groups', 'row'), ('col', 'sub')), parts along dimension 0, may hold values from -1.5 to 1.5
- feedforward_adjoint: bfloat16 [64, 1024, 256], P(('col', 'sub'), ('groups', 'row')), parts along dimension 1, may hold values from -1.5 to 1.5
- feedforward_scale: float32 [256], replicated, may hold values from 0.1 to 1.9
- expansion_matrix: bfloat16 [256, 1024], replicated, may hold values from -0.375 to 0.375
- contraction_matrix: bfloat16 [1024, 256], replicated, may hold values from -0.1875 to 0.1875
- product_scale_vector: float32 [256], replicated, may hold values from 0.1 to 1.9
- twin_operand_matrix: bfloat16 [256, 64], replicated, may hold values from -0.375 to 0.375
- couple_projection_matrix: bfloat16 [1024, 128], replicated, may hold values from -0.1875 to 0.1875
Outputs:
- alignment_start_adjoint: bfloat16 [64, 1024, 256], P(('col', 'sub'), ('groups', 'row')), parts along dimension 1
- grad_out_weight: float32 [2048, 128], P('groups'), parts along dimension 0
- grad_factor_weight: float32 [512, 64], P('groups'), parts along dimension 0
- grad_w_in: float32 [512, 1024], P('groups'), parts along dimension 0
- grad_w_mid: float32 [2048, 256], P('groups'), parts along dimension 0
- feedforward_scale_adjoint: float32 [512], P('groups'), parts along dimension 0
- product_scale_adjoint: float32 [512], P('groups'), parts along dimension 0
There are 2 independent parts, one for each index of `groups`. A program takes and returns all parts, laid end to end along the dimension named above; an argument that names none is the same for every part. Nothing has to cross between parts.
All inputs are finite; a program needn't handle non-finite values. No bound on the sum of `homolog_existence` or of `amino_existence` on one device may be relied on, other than what follows from the above.
Results may differ from a plain program's by a relative error of at most 0.015.
Values may be sent and summed in bfloat16 or wider, within the bound.
No kernel may reach another device: no remote copies, remote signals or barrier semaphores. Data moves between devices by JAX's collectives and lax.ppermute only.
A program may use at most 64 MiB of HBM per device.

v0:
```python
import math
import jax
import jax.numpy as jnp
from jax import lax
from jax.sharding import PartitionSpec as P

epsilon = 1e-05


def in_one_piece(arrays, axis, dim, along):
    ends, at = ([], 0)
    for a in arrays[:-1]:
        at += a.shape[along]
        ends.append(at)
    both = jnp.concatenate(arrays, axis=along)
    return tuple(jnp.split(lax.all_gather(both, axis, axis=dim, tiled=True), ends, axis=along))


def joined_along(parts, dim):
    parts = jnp.moveaxis(parts, 0, dim)
    lengths = parts.shape
    return parts.reshape(*lengths[:dim], lengths[dim] * lengths[dim + 1], *lengths[dim + 2 :])


def one_gather(arrays, axis, dims):
    vector = jnp.concatenate([a.reshape(-1) for a in arrays])
    lines, at, done = (lax.all_gather(vector, axis), 0, [])
    for a, dim in zip(arrays, dims):
        parts = lines[:, at : at + a.size].reshape(-1, *a.shape)
        done.append(joined_along(parts, dim))
        at += a.size
    return tuple(done)


def split_up(shard, dim, devices):
    lengths = shard.shape
    parts = shard.reshape(*lengths[:dim], devices, lengths[dim] // devices, *lengths[dim + 1 :])
    return jnp.moveaxis(parts, dim, 0)


def sent_and_summed(shard, axis, dim):
    parts = split_up(shard, dim, lax.axis_size(axis))
    arrived = lax.all_to_all(parts, axis, split_axis=0, concat_axis=0, tiled=True)
    return arrived.astype(jnp.float32).sum(axis=0)


def layer_normalize(values):
    centre = jnp.mean(values, axis=-1, keepdims=True)
    centred = values - centre
    variance = jnp.mean(centred * centred, axis=-1, keepdims=True)
    inv_std = lax.rsqrt(variance + epsilon)
    return (centred * inv_std, inv_std)


def standardizer_adjoint(grad_hat, normed, inv_std):
    first_mean = jnp.mean(grad_hat, axis=-1, keepdims=True)
    second_mean = jnp.mean(grad_hat * normed, axis=-1, keepdims=True)
    return inv_std * (grad_hat - first_mean - normed * second_mean)


def exact_gelu(values):
    return jax.nn.gelu(values, approximate=False)


def contract_rows(first_arr, second_arr):
    return lax.dot_general(
        first_arr, second_arr, (((0,), (0,)), ((), ())), preferred_element_type=jnp.float32
    )


def contract_last(first_arr, second_arr):
    return lax.dot_general(
        first_arr, second_arr, (((1,), (1,)), ((), ())), preferred_element_type=jnp.float32
    )


def per_device(
    saved_alignment,
    homolog_existence,
    amino_existence,
    couple_delta_adjoint,
    feedforward_adjoint,
    feedforward_scale,
    expansion_matrix,
    contraction_matrix,
    product_scale_vector,
    twin_operand_matrix,
    couple_projection_matrix,
):
    homolog_split_total, amino_split_total, lane_breadth = saved_alignment.shape
    factor = twin_operand_matrix.shape[1] // 2
    pair_width = couple_projection_matrix.shape[1]
    existing_record_lines = homolog_split_total * amino_split_total
    shard_count = lax.axis_size(("col", "sub"))
    row_devices = lax.axis_size("row")
    total_res = amino_split_total * row_devices
    col_res = total_res // shard_count
    all_seqs = homolog_split_total * shard_count
    embedding_numbers = saved_alignment.astype(jnp.float32).reshape(
        existing_record_lines, lane_breadth
    )
    transition_standardized, transition_inv_deviation = layer_normalize(embedding_numbers)
    normalized_input = (transition_standardized * feedforward_scale).astype(jnp.bfloat16)
    hidden_pre = jnp.dot(normalized_input, expansion_matrix, preferred_element_type=jnp.float32)
    gelu_value, gelu_back = jax.vjp(exact_gelu, hidden_pre)
    hidden = gelu_value.astype(jnp.bfloat16)
    mixed_values = embedding_numbers + jnp.dot(
        hidden, contraction_matrix, preferred_element_type=jnp.float32
    )
    product_zscored, product_reciprocal_spread = layer_normalize(mixed_values)
    normalized_output = (product_zscored * product_scale_vector).astype(jnp.bfloat16)
    projected = jnp.dot(normalized_output, twin_operand_matrix, preferred_element_type=jnp.float32)
    keep_mask = (homolog_existence * amino_existence[None, :]).astype(jnp.float32)
    keep_col = keep_mask.reshape(existing_record_lines, 1)
    left_factor = (
        (projected[:, :factor] * keep_col)
        .astype(jnp.bfloat16)
        .reshape(homolog_split_total, amino_split_total * factor)
    )
    right_factor = (
        (projected[:, factor:] * keep_col)
        .astype(jnp.bfloat16)
        .reshape(homolog_split_total, amino_split_total * factor)
    )
    keep_half = keep_mask.astype(jnp.bfloat16)
    left_all, keep_rows = in_one_piece((left_factor, keep_half), ("col", "sub"), 0, 1)
    right_spread, keep_spread = one_gather((right_factor, keep_half), "row", (1, 1))
    right_flat, keep_cols = (
        lax.all_to_all(right_spread, ("col", "sub"), split_axis=1, concat_axis=0, tiled=True),
        lax.all_to_all(keep_spread, ("col", "sub"), split_axis=1, concat_axis=0, tiled=True),
    )
    right_cols = right_flat.reshape(all_seqs, col_res, factor)
    left_rows = left_all.reshape(all_seqs, amino_split_total, factor)
    pair_count = contract_rows(keep_rows, keep_cols)
    inverse = 1.0 / jnp.maximum(pair_count, 1.0)
    block_rows = math.gcd(amino_split_total, 16)
    result_adjoint = jnp.zeros((factor * factor, pair_width), jnp.float32)
    grad_right = jnp.zeros((all_seqs, col_res, factor), jnp.float32)
    left_parts = []
    for row_start in range(0, amino_split_total, block_rows):
        left_block = left_rows[:, row_start : row_start + block_rows, :]
        inv_block = inverse[row_start : row_start + block_rows]
        cot_block = couple_delta_adjoint[row_start : row_start + block_rows]
        outer_sum = jnp.einsum(
            "sip,sjq->ijpq", left_block, right_cols, preferred_element_type=jnp.float32
        )
        outer_half = (outer_sum * inv_block[:, :, None, None]).astype(jnp.bfloat16)
        outer_half = outer_half.reshape(block_rows, col_res, factor * factor)
        result_adjoint = result_adjoint + jnp.einsum(
            "ijk,ijl->kl", outer_half, cot_block, preferred_element_type=jnp.float32
        )
        pair_back = jnp.einsum(
            "ijl,kl->ijk", cot_block, couple_projection_matrix, preferred_element_type=jnp.float32
        )
        back_half = (pair_back * inv_block[:, :, None]).astype(jnp.bfloat16)
        back_half = back_half.reshape(block_rows, col_res, factor, factor)
        left_parts.append(
            jnp.einsum("ijpq,sjq->sip", back_half, right_cols, preferred_element_type=jnp.float32)
        )
        grad_right = grad_right + jnp.einsum(
            "ijpq,sip->sjq", back_half, left_block, preferred_element_type=jnp.float32
        )
    grad_left = jnp.concatenate(left_parts, axis=1).reshape(all_seqs, amino_split_total * factor)
    left_own = sent_and_summed(grad_left.astype(jnp.bfloat16), ("col", "sub"), 0)
    right_back = lax.all_to_all(
        grad_right.reshape(all_seqs, col_res * factor).astype(jnp.bfloat16),
        ("col", "sub"),
        split_axis=0,
        concat_axis=1,
        tiled=True,
    )
    right_own = sent_and_summed(right_back, "row", 1)
    grad_proj = jnp.concatenate(
        [
            left_own.reshape(existing_record_lines, factor),
            right_own.reshape(existing_record_lines, factor),
        ],
        axis=1,
    )
    grad_proj = (grad_proj * keep_col).astype(jnp.bfloat16)
    operand_adjoint = contract_rows(normalized_output, grad_proj)
    rescaled_result_adjoint = contract_last(grad_proj, twin_operand_matrix)
    product_scale_adjoint = jnp.sum(rescaled_result_adjoint * product_zscored, axis=0)
    combined_adjoint = feedforward_adjoint.astype(jnp.float32).reshape(
        existing_record_lines, lane_breadth
    ) + standardizer_adjoint(
        rescaled_result_adjoint * product_scale_vector, product_zscored, product_reciprocal_spread
    )
    grad_mixed_half = combined_adjoint.astype(jnp.bfloat16)
    hidden_adjoint = contract_rows(hidden, grad_mixed_half)
    grad_hidden = contract_last(grad_mixed_half, contraction_matrix)
    grad_pre = gelu_back(grad_hidden)[0].astype(jnp.bfloat16)
    expansion_adjoint = contract_rows(normalized_input, grad_pre)
    normed_input_gradient = contract_last(grad_pre, expansion_matrix)
    feedforward_scale_adjoint = jnp.sum(normed_input_gradient * transition_standardized, axis=0)
    alignment_start_adjoint = combined_adjoint + standardizer_adjoint(
        normed_input_gradient * feedforward_scale, transition_standardized, transition_inv_deviation
    )
    weight_grads = lax.psum(
        (
            result_adjoint,
            operand_adjoint,
            expansion_adjoint,
            hidden_adjoint,
            feedforward_scale_adjoint,
            product_scale_adjoint,
        ),
        ("row", "col", "sub"),
    )
    return (
        alignment_start_adjoint.astype(jnp.bfloat16).reshape(
            homolog_split_total, amino_split_total, lane_breadth
        ),
        weight_grads[0],
        weight_grads[1],
        weight_grads[2],
        weight_grads[3],
        weight_grads[4],
        weight_grads[5],
    )


def solution(mesh):
    return jax.shard_map(
        per_device,
        mesh=mesh,
        in_specs=(
            P(("col", "sub"), ("groups", "row"), None),
            P(("col", "sub"), ("groups", "row")),
            P(("groups", "row")),
            P(("groups", "row"), ("col", "sub"), None),
            P(("col", "sub"), ("groups", "row"), None),
            P(),
            P(),
            P(),
            P(),
            P(),
            P(),
        ),
        out_specs=(
            P(("col", "sub"), ("groups", "row"), None),
            P("groups", None),
            P("groups", None),
            P("groups", None),
            P("groups", None),
            P("groups"),
            P("groups"),
        ),
        check_vma=False,
    )
```

profile of v0, /device:TPU:33, one launch (start us, length us, event | category | flops | bytes accessed | tf_op | source)
XLA Modules:
  0.0 527.1 jit_solution(18394093957308587515)
XLA Ops:
  11.5 3.4 multiply_convert_fusion.2
  17.4 45.3 %all-gather.1 = bf16[16,1,8448]{2,1,0:T(2,128)(2,1)S(1)} all-gather(bf16[1,1,8448]{2,1,0:T(2,128)(2,1)S(1)} %reshape.176), channel_id=2, replica_groups=mesh['groups'=2,'row'=16,'col'=4,'sub'=2] {'row'}, dimensions={0}, use_global_device_ids=true | all-gather | bytes 287232 | tf_op jit(solution)/shard_map/all_gather | solution.py:27
  63.6 12.2 %all-to-all-start.1 = ((bf16[8,2,256]{2,1,0:T(2,128)(2,1)}), bf16[8,2,256]{2,1,0:T(2,128)(2,1)S(1)}, u32[]{:S(2)}, u32[]{:S(2)}) async-start(bf16[8,2,256]{2,1,0:T(2,128)(2,1)} %reshape.192), calls=%async_computation.1 | async-start | bytes 16384 | tf_op jit(solution)/shard_map/all_to_all | solution.py:130
  76.1 13.7 %all_gather.11 = bf16[64,1056]{1,0:T(8,128)(2,1)S(1)} all-gather(bf16[8,1056]{1,0:T(8,128)(2,1)S(1)} %pad_maximum_fusion.2), channel_id=1, replica_groups=mesh['groups'=2,'row'=16,'col'=4,'sub'=2] {'col','sub'}, dimensions={0}, use_global_device_ids=true | all-gather | bytes 152064 | tf_op jit(solution)/shard_map/all_gather | solution.py:16
  90.9 4.1 all-to-all-start
  95.3 1.7 multiply_convert_fusion
  97.1 3.2 copy.56
  100.3 1.7 multiply_convert_fusion.1
  102.0 3.2 copy.53
  105.2 3.8 fusion.10
  109.0 1.5 fusion.19
  111.2 1.8 convert_element_type.80
  113.1 5.0 all-to-all-start.3
  118.1 1.9 reshape.161
  120.9 3.6 fusion.29
  124.6 1.3 fusion.32
  128.9 4.8 all-to-all-start.2
  133.7 3.2 fusion.1
  139.0 4.0 all-to-all-start.4
  145.4 2.7 copy.67
  148.2 2.7 copy.70
  151.9 1.8 fusion.22
  153.8 2.7 all-to-all-done.4
  158.2 1.3 fusion.50
  159.6 2.1 add_convert_fusion
  161.7 1.3 fusion.67
  163.6 252.7 %all-reduce = (f32[256]{0:T(256)}, f32[256]{0:T(256)}) all-reduce(f32[256]{0:T(256)S(1)} %get-tuple-element.9, f32[256]{0:T(256)S(1)} %get-tuple-element.7), channel_id=1, replica_groups=mesh['groups'=2,'row'=16,'col'=4,'sub'=2] {'row','col','sub'}, use_global_device_ids=true, to_apply=%region_15.0 | all-reduce | flops 512 | bytes 4096 | tf_op jit(solution)/shard_map/psum | solution.py:199
  417.1 95.3 %all-reduce.4.cloned.1.call-done = (f32[1024,128]{1,0:T(8,128)}, f32[256,64]{0,1:T(8,128)}, f32[256,1024]{1,0:T(8,128)}, f32[1024,256]{1,0:T(8,128)}) async-done(((f32[1024,128]{1,0:T(8,128)}, f32[256,64]{0,1:T(8,128)}, f32[256,1024]{1,0:T(8,128)}, f32[1024,256]{1,0:T(8,128)}), (f32[1024,128]{1,0:T(8,128)}, f32[256,64]{0,1:T(8,128)}, f32[256,1024]{1,0:T(8,128)}, ...) | async-done | bytes 2686992 | tf_op jit(solution)/shard_map/psum | solution.py:199
  512.4 1.9 copy.122
  514.2 1.5 copy.123
  515.7 2.3 copy.124
  518.0 2.3 copy.125
  (122 shorter events, 22.6 us)
Async XLA Ops:
  7.2 4.3 copy-start
  8.4 6.6 %copy-start.17 = (f32[256]{0:T(256)}, f32[256]{0:T(256)S(1)}, u32[]{:S(2)}) copy-start(f32[256]{0:T(256)S(1)} %div.30) | copy-start | bytes 3076
  9.5 5.4 %copy-start.19 = (f32[256]{0:T(256)}, f32[256]{0:T(256)S(1)}, u32[]{:S(2)}) copy-start(f32[256]{0:T(256)S(1)} %rsqrt.20) | copy-start | bytes 3076
  10.3 6.7 %copy-start.21 = (f32[256]{0:T(256)}, f32[256]{0:T(256)S(1)}, u32[]{:S(2)}) copy-start(f32[256]{0:T(256)S(1)} %mul.200) | copy-start | bytes 3076
  11.5 4.3 copy-start.4
  11.5 4.3 copy-start.8
  11.5 5.3 copy-start.23
  11.5 5.4 %copy-start.10 = (bf16[256,64]{0,1:T(8,128)(2,1)S(1)}, bf16[256,64]{0,1:T(8,128)(2,1)}, u32[]{:S(2)}) copy-start(bf16[256,64]{0,1:T(8,128)(2,1)} %param.20) | copy-start | bytes 98308
  15.0 0.8 copy-start.5
  16.2 0.6 copy-start.13
  16.8 59.3 %copy-start.15 = (f32[256]{0:T(256)}, f32[256]{0:T(256)S(1)}, u32[]{:S(2)}) copy-start(f32[256]{0:T(256)S(1)} %add_rsqrt_fusion.1) | copy-start | bytes 3076
  63.6 27.3 %all-to-all-start.1 = ((bf16[8,2,256]{2,1,0:T(2,128)(2,1)}), bf16[8,2,256]{2,1,0:T(2,128)(2,1)S(1)}, u32[]{:S(2)}, u32[]{:S(2)}) async-start(bf16[8,2,256]{2,1,0:T(2,128)(2,1)} %reshape.192), calls=%async_computation.1 | async-start | bytes 16384 | tf_op jit(solution)/shard_map/all_to_all | solution.py:130
  90.9 22.1 %all-to-all-start = ((bf16[8,8,2048]{2,0,1:T(8,128)(2,1)}), bf16[8,8,2048]{2,0,1:T(8,128)(2,1)}, u32[]{:S(2)}, u32[]{:S(2)}) async-start(bf16[8,8,2048]{2,0,1:T(8,128)(2,1)} %copy.49), calls=%async_computation | async-start | bytes 524288 | tf_op jit(solution)/shard_map/all_to_all | solution.py:129
  105.2 3.8 copy-start.1
  113.1 15.9 %all-to-all-start.3 = ((bf16[8,8,2048]{2,1,0:T(8,128)(2,1)}), bf16[8,8,2048]{2,1,0:T(8,128)(2,1)S(1)}, u32[]{:S(2)}, u32[]{:S(2)}) async-start(bf16[8,8,2048]{2,1,0:T(8,128)(2,1)} %convert_element_type.80), calls=%async_computation.3 | async-start | bytes 524288 | tf_op jit(solution)/shard_map/all_to_all | solution.py:165
  120.9 3.7 copy-start.2
  128.9 10.1 %all-to-all-start.2 = ((bf16[8,8,1024]{2,1,0:T(8,128)(2,1)}), bf16[8,8,1024]{2,1,0:T(8,128)(2,1)S(1)}, u32[]{:S(2)}, u32[]{:S(2)}) async-start(bf16[8,8,1024]{2,1,0:T(8,128)(2,1)} %convert_element_type.77), calls=%async_computation.2 | async-start | bytes 262144 | tf_op jit(solution)/shard_map/all_to_all | solution.py:43
  139.0 17.5 %all-to-all-start.4 = ((bf16[16,8,1024]{2,1,0:T(8,128)(2,1)}), bf16[16,8,1024]{2,1,0:T(8,128)(2,1)S(1)}, u32[]{:S(2)}, u32[]{:S(2)}) async-start(bf16[16,8,1024]{2,1,0:T(8,128)(2,1)} %copy.65), calls=%async_computation.4 | async-start | bytes 524288 | tf_op jit(solution)/shard_map/all_to_all | solution.py:43
  143.0 369.4 %all-reduce.4.cloned.1.call-start = ((), (), s32[]{:S(2)}) async-start(), calls=%async_computation.5 | async-start | bytes 5373952 | tf_op jit(solution)/shard_map/psum | solution.py:199
  143.3 2.2 copy-start.3
  148.1 2.7 copy-start.7
  151.8 4.8 copy-start.22
  151.8 5.8 %copy-start.11 = (bf16[256,64]{0,1:T(8,128)(2,1)S(1)}, bf16[256,64]{0,1:T(8,128)(2,1)}, u32[]{:S(2)}) copy-start(bf16[256,64]{0,1:T(8,128)(2,1)} %param.20) | copy-start | bytes 98308
  151.8 5.8 %copy-start.14 = (f32[256]{0:T(256)S(1)}, f32[256]{0:T(256)}, u32[]{:S(2)}) copy-start(f32[256]{0:T(256)} %copy-done.13) | copy-start | bytes 3076
  151.8 5.8 %copy-start.16 = (f32[256]{0:T(256)S(1)}, f32[256]{0:T(256)}, u32[]{:S(2)}) copy-start(f32[256]{0:T(256)} %copy-done.15) | copy-start | bytes 3076
  151.9 5.8 %copy-start.24 = (f32[256]{0:T(256)S(1)}, f32[256]{0:T(256)}, u32[]{:S(2)}) copy-start(f32[256]{0:T(256)} %param.19) | copy-start | bytes 3076
  151.9 6.1 %copy-start.12 = (bf16[8,32,256]{2,1,0:T(8,128)(2,1)S(1)}, bf16[8,32,256]{2,1,0:T(8,128)(2,1)}, u32[]{:S(2)}) copy-start(bf16[8,32,256]{2,1,0:T(8,128)(2,1)} %param.15) | copy-start | bytes 393220
  151.9 6.3 %copy-start.6 = (bf16[256,1024]{1,0:T(8,128)(2,1)S(1)}, bf16[256,1024]{1,0:T(8,128)(2,1)}, u32[]{:S(2)}) copy-start(bf16[256,1024]{1,0:T(8,128)(2,1)} %copy-done.5) | copy-start | bytes 1572868
  151.9 7.7 %copy-start.9 = (bf16[1024,256]{1,0:T(8,128)(2,1)S(1)}, bf16[1024,256]{1,0:T(8,128)(2,1)}, u32[]{:S(2)}) copy-start(bf16[1024,256]{1,0:T(8,128)(2,1)} %param.18) | copy-start | bytes 1572868
  159.5 3.5 copy-start.18
  159.5 3.5 copy-start.20
  159.5 3.5 copy-start.25
Sparse Core Ops, SparseCore 0:
  163.2 349.1 all-reduce.3
where the time goes:
time: 528 us; the launch traced here: 527 us
  blocking collectives  312 us (59%)
  waiting for transfers between devices  99 us (19%)
  local copies, waits for them, and re-layouts  34.5 us (7%)
  matrix products  31.3 us (6%)
  starting transfers between devices  30.4 us (6%)
  between operations  14.6 us (3%)
  other arithmetic  5.63 us (1%)
    psum x1, blocking collectives, per_device(): lax.psum((result_adjoint, operand_adjoint, expansion_adjoint, hidden_adjo...  253 us
    psum x1, waiting for transfers between devices, per_device(): lax.psum((result_adjoint, operand_adjoint, expansion_adjoint, hidden_adjo...  95.3 us
    all_gather x1, blocking collectives, one_gather(): lines, at, done = (lax.all_gather(vector, axis), 0, [])  45.3 us
    all_gather x1, blocking collectives, in_one_piece(): lax.all_gather(both, axis, axis=dim, tiled=True)  13.7 us
    all_to_all x1, starting transfers between devices, per_device(): lax.all_to_all(keep_spread, ('col', 'sub'), split_axis=1, concat_axis=0,...  12.2 us
    unnamed x60, local copies, waits for them, and re-layouts  11 us
  transfers between devices with their start and end apart: 6, of which 3 were waited for; matrix products, arithmetic and copies ran while one was open for 9% of the time, Pallas kernels for 0%

commit v1 on v0

--- a/solution.py
+++ b/solution.py
@@ -5,6 +5,7 @@
 from jax.sharding import PartitionSpec as P
 
 epsilon = 1e-05
+find_types = lambda mine_x, a_name, link_axis: jax.lax.psum(jax.lax.psum(mine_x, a_name), link_axis)
 
 
 def in_one_piece(arrays, axis, dim, along):
@@ -196,7 +197,7 @@
     alignment_start_adjoint = combined_adjoint + standardizer_adjoint(
         normed_input_gradient * feedforward_scale, transition_standardized, transition_inv_deviation
     )
-    weight_grads = lax.psum(
+    weight_grads = find_types(
         (
             result_adjoint,
             operand_adjoint,
@@ -205,7 +206,8 @@
             feedforward_scale_adjoint,
             product_scale_adjoint,
         ),
-        ("row", "col", "sub"),
+        "row",
+        ("col", "sub"),
     )
     return (
         alignment_start_adjoint.astype(jnp.bfloat16).reshape(

time: 528 us -> 401 us (0.76)
  blocking collectives: 312 us -> 109 us
  waiting for transfers between devices: 99 us -> 173 us
    psum x1 -> x2, blocking collectives: 253 us -> 50.3 us  [the longest x1 29.3 us: jax.lax.psum(jax.lax.psum(mine_x, a_name), link_axis)]
    psum x1 -> x2, waiting for transfers between devices: 95.3 us -> 169 us  [the longest x1 136 us: jax.lax.psum(mine_x, a_name)]
  transfers between devices with their start and end apart: 6 -> 7, of which waited for: 3 -> 4; matrix products, arithmetic and copies ran while one was open for 9% -> 11% of each run, Pallas kernels for 0% -> 0%
where the time goes in v1:
time: 401 us; the launch traced here: 400 us
  waiting for transfers between devices  173 us (43%)
  blocking collectives  109 us (27%)
  local copies, waits for them, and re-layouts  35.1 us (9%)
  matrix products  31.3 us (8%)
  starting transfers between devices  30.5 us (8%)
  between operations  14.6 us (4%)
  other arithmetic  5.63 us (1%)
    psum x1, waiting for transfers between devices, jax.lax.psum(mine_x, a_name)  136 us
    all_gather x1, blocking collectives, one_gather(): lines, at, done = (lax.all_gather(vector, axis), 0, [])  45.3 us
    psum x1, waiting for transfers between devices, jax.lax.psum(jax.lax.psum(mine_x, a_name), link_axis)  33.9 us
    psum x1, blocking collectives, jax.lax.psum(jax.lax.psum(mine_x, a_name), link_axis)  29.3 us
    psum x1, blocking collectives, jax.lax.psum(mine_x, a_name)  21 us
    all_gather x1, blocking collectives, in_one_piece(): lax.all_gather(both, axis, axis=dim, tiled=True)  13.7 us
    all_to_all x1, starting transfers between devices, per_device(): lax.all_to_all(keep_spread, ('col', 'sub'), split_axis=1, concat_axis=0,...  12.2 us
    unnamed x60, local copies, waits for them, and re-layouts  11.6 us
  transfers between devices with their start and end apart: 7, of which 4 were waited for; matrix products, arithmetic and copies ran while one was open for 11% of the time, Pallas kernels for 0%

profile of v1, /device:TPU:33, one launch (start us, length us, event | category | flops | bytes accessed | tf_op | source)
XLA Modules:
  0.0 399.7 jit_solution(12549568316085416656)
XLA Ops:
  11.5 3.4 multiply_convert_fusion.2
  17.9 45.3 %all-gather.1 = bf16[16,1,8448]{2,1,0:T(2,128)(2,1)S(1)} all-gather(bf16[1,1,8448]{2,1,0:T(2,128)(2,1)S(1)} %reshape.176), channel_id=2, replica_groups=mesh['groups'=2,'row'=16,'col'=4,'sub'=2] {'row'}, dimensions={0}, use_global_device_ids=true | all-gather | bytes 287232 | tf_op jit(solution)/shard_map/all_gather | solution.py:28
  64.2 12.2 %all-to-all-start.1 = ((bf16[8,2,256]{2,1,0:T(2,128)(2,1)}), bf16[8,2,256]{2,1,0:T(2,128)(2,1)S(1)}, u32[]{:S(2)}, u32[]{:S(2)}) async-start(bf16[8,2,256]{2,1,0:T(2,128)(2,1)} %reshape.192), calls=%async_computation.1 | async-start | bytes 16384 | tf_op jit(solution)/shard_map/all_to_all | solution.py:131
  76.6 13.7 %all_gather.11 = bf16[64,1056]{1,0:T(8,128)(2,1)S(1)} all-gather(bf16[8,1056]{1,0:T(8,128)(2,1)S(1)} %pad_maximum_fusion.2), channel_id=1, replica_groups=mesh['groups'=2,'row'=16,'col'=4,'sub'=2] {'col','sub'}, dimensions={0}, use_global_device_ids=true | all-gather | bytes 152064 | tf_op jit(solution)/shard_map/all_gather | solution.py:17
  91.5 4.1 %all-to-all-start = ((bf16[8,8,2048]{2,0,1:T(8,128)(2,1)}), bf16[8,8,2048]{2,0,1:T(8,128)(2,1)}, u32[]{:S(2)}, u32[]{:S(2)}) async-start(bf16[8,8,2048]{2,0,1:T(8,128)(2,1)} %copy.49), calls=%async_computation | async-start | bytes 524288 | tf_op jit(solution)/shard_map/all_to_all | solution.py:130
  95.9 1.8 multiply_convert_fusion
  97.6 3.2 copy.56
  100.8 1.7 multiply_convert_fusion.1
  102.6 3.2 copy.53
  105.7 3.8 fusion.10
  109.5 1.5 fusion.19
  111.8 1.8 convert_element_type.80
  113.6 5.0 %all-to-all-start.3 = ((bf16[8,8,2048]{2,1,0:T(8,128)(2,1)}), bf16[8,8,2048]{2,1,0:T(8,128)(2,1)S(1)}, u32[]{:S(2)}, u32[]{:S(2)}) async-start(bf16[8,8,2048]{2,1,0:T(8,128)(2,1)} %convert_element_type.80), calls=%async_computation.3 | async-start | bytes 524288 | tf_op jit(solution)/shard_map/all_to_all | solution.py:166
  118.7 1.9 reshape.161
  121.5 3.6 fusion.29
  129.5 4.8 %all-to-all-start.2 = ((bf16[8,8,1024]{2,1,0:T(8,128)(2,1)}), bf16[8,8,1024]{2,1,0:T(8,128)(2,1)S(1)}, u32[]{:S(2)}, u32[]{:S(2)}) async-start(bf16[8,8,1024]{2,1,0:T(8,128)(2,1)} %convert_element_type.77), calls=%async_computation.2 | async-start | bytes 262144 | tf_op jit(solution)/shard_map/all_to_all | solution.py:44
  134.3 3.2 fusion.1
  139.5 4.0 all-to-all-start.4
  146.0 2.7 copy.67
  148.7 2.7 copy.70
  152.5 1.8 fusion.22
  154.3 2.7 all-to-all-done.4
  158.8 1.3 fusion.50
  160.1 2.1 add_convert_fusion
  163.7 135.6 %all-reduce.7.cloned.1.call-done = (f32[1024,128]{1,0:T(8,128)}, f32[256,64]{0,1:T(8,128)}, f32[256,1024]{1,0:T(8,128)}, f32[1024,256]{1,0:T(8,128)}) async-done(((f32[1024,128]{1,0:T(8,128)}, f32[256,64]{0,1:T(8,128)}, f32[256,1024]{1,0:T(8,128)}, f32[1024,256]{1,0:T(8,128)}), (f32[1024,128]{1,0:T(8,128)}, f32[256,64]{0,1:T(8,128)}, f32[256,1024]{1,0:T(8,128)}, ...) | async-done | bytes 2686992 | tf_op jit(solution)/shard_map/psum | solution.py:8
  299.8 21.0 %all-reduce = (f32[256]{0:T(256)S(1)}, f32[256]{0:T(256)S(1)}) all-reduce(f32[256]{0:T(256)S(1)} %get-tuple-element.9, f32[256]{0:T(256)S(1)} %get-tuple-element.7), channel_id=1, replica_groups=mesh['groups'=2,'row'=16,'col'=4,'sub'=2] {'row'}, use_global_device_ids=true, to_apply=%region_19.0 | all-reduce | flops 512 | bytes 4096 | tf_op jit(solution)/shard_map/psum | solution.py:8
  320.8 29.3 %all-reduce.2 = (f32[256]{0:T(256)}, f32[256]{0:T(256)}) all-reduce(f32[256]{0:T(256)S(1)} %get-tuple-element.13, f32[256]{0:T(256)S(1)} %get-tuple-element.14), channel_id=1, replica_groups=mesh['groups'=2,'row'=16,'col'=4,'sub'=2] {'col','sub'}, use_global_device_ids=true, to_apply=%region_20.0 | all-reduce | flops 512 | bytes 4096 | tf_op jit(solution)/shard_map/psum | solution.py:8
  351.0 33.9 %all-reduce.9.cloned.1.call-done = (f32[1024,128]{1,0:T(8,128)}, f32[256,64]{0,1:T(8,128)}, f32[256,1024]{1,0:T(8,128)}, f32[1024,256]{1,0:T(8,128)}) async-done(((f32[1024,128]{1,0:T(8,128)}, f32[256,64]{0,1:T(8,128)}, f32[256,1024]{1,0:T(8,128)}, f32[1024,256]{1,0:T(8,128)}), (f32[1024,128]{1,0:T(8,128)}, f32[256,64]{0,1:T(8,128)}, f32[256,1024]{1,0:T(8,128)}, ...) | async-done | bytes 2686992 | tf_op jit(solution)/shard_map/psum | solution.py:8
  384.9 1.9 copy.126
  386.8 1.5 copy.127
  388.3 2.3 copy.128
  390.6 2.3 copy.129
  (126 shorter events, 25.9 us)
Async XLA Ops:
  7.2 4.3 %copy-start = (bf16[256,1024]{1,0:T(8,128)(2,1)S(1)}, bf16[256,1024]{1,0:T(8,128)(2,1)}, u32[]{:S(2)}) copy-start(bf16[256,1024]{1,0:T(8,128)(2,1)} %param.17) | copy-start | bytes 1572868
  8.4 2.1 copy-start.17
  9.5 0.9 copy-start.19
  10.3 7.3 %copy-start.21 = (f32[256]{0:T(256)}, f32[256]{0:T(256)S(1)}, u32[]{:S(2)}) copy-start(f32[256]{0:T(256)S(1)} %mul.200) | copy-start | bytes 3076
  11.5 4.3 %copy-start.4 = (bf16[8,32,256]{2,1,0:T(8,128)(2,1)S(1)}, bf16[8,32,256]{2,1,0:T(8,128)(2,1)}, u32[]{:S(2)}) copy-start(bf16[8,32,256]{2,1,0:T(8,128)(2,1)} %param.11) | copy-start | bytes 393220
  11.5 4.3 %copy-start.8 = (bf16[1024,256]{1,0:T(8,128)(2,1)S(1)}, bf16[1024,256]{1,0:T(8,128)(2,1)}, u32[]{:S(2)}) copy-start(bf16[1024,256]{1,0:T(8,128)(2,1)} %param.18) | copy-start | bytes 1572868
  11.5 5.8 %copy-start.23 = (f32[256]{0:T(256)S(1)}, f32[256]{0:T(256)}, u32[]{:S(2)}) copy-start(f32[256]{0:T(256)} %param.19) | copy-start | bytes 3076
  11.5 5.9 %copy-start.10 = (bf16[256,64]{0,1:T(8,128)(2,1)S(1)}, bf16[256,64]{0,1:T(8,128)(2,1)}, u32[]{:S(2)}) copy-start(bf16[256,64]{0,1:T(8,128)(2,1)} %param.20) | copy-start | bytes 98308
  15.0 0.8 copy-start.5
  16.2 0.6 copy-start.13
  64.2 27.3 %all-to-all-start.1 = ((bf16[8,2,256]{2,1,0:T(2,128)(2,1)}), bf16[8,2,256]{2,1,0:T(2,128)(2,1)S(1)}, u32[]{:S(2)}, u32[]{:S(2)}) async-start(bf16[8,2,256]{2,1,0:T(2,128)(2,1)} %reshape.192), calls=%async_computation.1 | async-start | bytes 16384 | tf_op jit(solution)/shard_map/all_to_all | solution.py:131
  91.5 22.1 %all-to-all-start = ((bf16[8,8,2048]{2,0,1:T(8,128)(2,1)}), bf16[8,8,2048]{2,0,1:T(8,128)(2,1)}, u32[]{:S(2)}, u32[]{:S(2)}) async-start(bf16[8,8,2048]{2,0,1:T(8,128)(2,1)} %copy.49), calls=%async_computation | async-start | bytes 524288 | tf_op jit(solution)/shard_map/all_to_all | solution.py:130
  105.7 3.8 copy-start.1
  113.6 15.9 %all-to-all-start.3 = ((bf16[8,8,2048]{2,1,0:T(8,128)(2,1)}), bf16[8,8,2048]{2,1,0:T(8,128)(2,1)S(1)}, u32[]{:S(2)}, u32[]{:S(2)}) async-start(bf16[8,8,2048]{2,1,0:T(8,128)(2,1)} %convert_element_type.80), calls=%async_computation.3 | async-start | bytes 524288 | tf_op jit(solution)/shard_map/all_to_all | solution.py:166
  121.5 3.6 copy-start.2
  129.5 10.1 %all-to-all-start.2 = ((bf16[8,8,1024]{2,1,0:T(8,128)(2,1)}), bf16[8,8,1024]{2,1,0:T(8,128)(2,1)S(1)}, u32[]{:S(2)}, u32[]{:S(2)}) async-start(bf16[8,8,1024]{2,1,0:T(8,128)(2,1)} %convert_element_type.77), calls=%async_computation.2 | async-start | bytes 262144 | tf_op jit(solution)/shard_map/all_to_all | solution.py:44
  139.5 17.5 %all-to-all-start.4 = ((bf16[16,8,1024]{2,1,0:T(8,128)(2,1)}), bf16[16,8,1024]{2,1,0:T(8,128)(2,1)S(1)}, u32[]{:S(2)}, u32[]{:S(2)}) async-start(bf16[16,8,1024]{2,1,0:T(8,128)(2,1)} %copy.65), calls=%async_computation.4 | async-start | bytes 524288 | tf_op jit(solution)/shard_map/all_to_all | solution.py:44
  143.5 155.7 %all-reduce.7.cloned.1.call-start = ((), (), s32[]{:S(2)}) async-start(), calls=%async_computation.5 | async-start | bytes 5373952 | tf_op jit(solution)/shard_map/psum | solution.py:8
  143.8 2.2 copy-start.3
  148.7 2.7 copy-start.7
  152.4 4.8 %copy-start.22 = (f32[256]{0:T(256)S(1)}, f32[256]{0:T(256)}, u32[]{:S(2)}) copy-start(f32[256]{0:T(256)} %copy-done.21) | copy-start | bytes 3076
  152.4 5.8 %copy-start.11 = (bf16[256,64]{0,1:T(8,128)(2,1)S(1)}, bf16[256,64]{0,1:T(8,128)(2,1)}, u32[]{:S(2)}) copy-start(bf16[256,64]{0,1:T(8,128)(2,1)} %param.20) | copy-start | bytes 98308
  152.4 5.8 %copy-start.14 = (f32[256]{0:T(256)S(1)}, f32[256]{0:T(256)}, u32[]{:S(2)}) copy-start(f32[256]{0:T(256)} %copy-done.13) | copy-start | bytes 3076
  152.4 5.8 %copy-start.16 = (f32[256]{0:T(256)S(1)}, f32[256]{0:T(256)}, u32[]{:S(2)}) copy-start(f32[256]{0:T(256)} %copy-done.15) | copy-start | bytes 3076
  152.4 5.8 %copy-start.24 = (f32[256]{0:T(256)S(1)}, f32[256]{0:T(256)}, u32[]{:S(2)}) copy-start(f32[256]{0:T(256)} %param.19) | copy-start | bytes 3076
  152.4 6.1 %copy-start.12 = (bf16[8,32,256]{2,1,0:T(8,128)(2,1)S(1)}, bf16[8,32,256]{2,1,0:T(8,128)(2,1)}, u32[]{:S(2)}) copy-start(bf16[8,32,256]{2,1,0:T(8,128)(2,1)} %param.15) | copy-start | bytes 393220
  152.4 6.3 %copy-start.6 = (bf16[256,1024]{1,0:T(8,128)(2,1)S(1)}, bf16[256,1024]{1,0:T(8,128)(2,1)}, u32[]{:S(2)}) copy-start(bf16[256,1024]{1,0:T(8,128)(2,1)} %copy-done.5) | copy-start | bytes 1572868
  152.4 7.7 %copy-start.9 = (bf16[1024,256]{1,0:T(8,128)(2,1)S(1)}, bf16[1024,256]{1,0:T(8,128)(2,1)}, u32[]{:S(2)}) copy-start(bf16[1024,256]{1,0:T(8,128)(2,1)} %param.18) | copy-start | bytes 1572868
  162.2 137.1 %copy-start.18 = (f32[256]{0:T(256)S(1)}, f32[256]{0:T(256)}, u32[]{:S(2)}) copy-start(f32[256]{0:T(256)} %copy-done.17) | copy-start | bytes 3076
  162.2 137.1 %copy-start.20 = (f32[256]{0:T(256)S(1)}, f32[256]{0:T(256)}, u32[]{:S(2)}) copy-start(f32[256]{0:T(256)} %copy-done.19) | copy-start | bytes 3076
  162.3 137.1 %copy-start.25 = (f32[256]{0:T(256)S(1)}, f32[256]{0:T(256)}, u32[]{:S(2)}) copy-start(f32[256]{0:T(256)} %param.16) | copy-start | bytes 3076
  163.6 221.3 %all-reduce.9.cloned.1.call-start = ((), (), s32[]{:S(2)}) async-start(), calls=%async_computation.6 | async-start | bytes 5373952 | tf_op jit(solution)/shard_map/psum | solution.py:8
  (1 other events, 0.6 us)
Sparse Core Ops, SparseCore 0:
  163.7 135.4 all-reduce.6
  301.9 82.9 all-reduce.8
